TPU v7x, 32 devices: a whole 2x2x4 slice. The times are simulated.
32 devices in a mesh: row: 4 (over x, core), col: 8 (over z, y).
Axes of the slice: x: 2, y: 2, z: 4, core: 2. Of those that a mesh axis runs over, the one named last changes fastest.
Arguments:
- x_rows: float32 [16, 16384], P(None, ('row', 'col')), may hold values from -6 to 6
- alpha_rows: float32 [16384], P(('row', 'col')), may hold values from -0.5 to 1.5
- x_cols: float32 [16, 8192], P(None, ('col', 'row')), may hold values from -6 to 6
- alpha_cols: float32 [8192], P(('col', 'row')), may hold values from -0.0073242188 to 0.021972656
- lengthscale: float32 [16], replicated, may hold values from 1.2 to 2.5
Outputs:
- row_terms: float32 [16, 16384], P(None, ('row', 'col'))
- kernel_alpha: float32 [16384], P(('row', 'col'))
- grad: float32 [16], replicated
All inputs are finite; a program needn't handle non-finite values.
Results may differ from a plain program's by a relative error of at most 0.00021.
Values sent between devices are 32-bit elements; how exact they have to be, the bound alone decides.
A program may use at most 64 MiB of HBM per device.

v0:
```python
import jax
import jax.numpy as jnp
from jax import lax
from jax.sharding import PartitionSpec as P


def fold_terms(partials, row_scaled, row_alpha):
    dims = row_scaled.shape[0]
    weight_sum = partials[0]
    first_moment = partials[1 : 1 + dims]
    second_moment = partials[1 + dims :]
    terms = (
        0.5
        * row_alpha[None, :]
        * (
            row_scaled * row_scaled * weight_sum[None, :]
            - 2.0 * row_scaled * first_moment
            + second_moment
        )
    )
    return (terms, weight_sum)


def on_device(x_rows, alpha_rows, x_cols, alpha_cols, lengthscale):
    dims = x_rows.shape[0]
    inverse_scale = 1.0 / lengthscale
    own_scaled = x_rows * inverse_scale[:, None]
    own_rows = jnp.concatenate([own_scaled, alpha_rows[None, :]], 0)
    gathered = lax.all_gather(own_rows, "col", axis=1, tiled=True)
    row_scaled = gathered[:dims]
    row_alpha = gathered[dims]
    row_count = row_scaled.shape[1]
    block_rows = min(512, row_count)
    block_count = row_count // block_rows
    row_norms = jnp.sum(row_scaled * row_scaled, 0)
    own_cols = jnp.concatenate([x_cols * inverse_scale[:, None], alpha_cols[None, :]], 0)
    empty = jnp.zeros((2 * dims + 1, row_count), jnp.float32)
    shard_piece = lax.all_gather(own_cols, "row", axis=1, tiled=True)
    col_scaled = shard_piece[:dims]
    col_alpha = shard_piece[dims]
    col_norms = jnp.sum(col_scaled * col_scaled, 0)
    values = jnp.concatenate(
        [
            col_alpha[None, :],
            col_alpha[None, :] * col_scaled,
            col_alpha[None, :] * col_scaled * col_scaled,
        ],
        0,
    )

    def add_block(block_index, carried):
        offset = block_index * block_rows
        row_block = lax.dynamic_slice_in_dim(row_scaled, offset, block_rows, 1)
        block_norms = lax.dynamic_slice_in_dim(row_norms, offset, block_rows, 0)
        cross = lax.dot_general(
            row_block,
            col_scaled,
            (((0,), (0,)), ((), ())),
            precision=lax.Precision.HIGHEST,
            preferred_element_type=jnp.float32,
        )
        kernel = jnp.exp(-0.5 * (block_norms[:, None] + col_norms[None, :] - 2.0 * cross))
        contrib = lax.dot_general(
            values,
            kernel,
            (((1,), (1,)), ((), ())),
            precision=lax.Precision.HIGHEST,
            preferred_element_type=jnp.float32,
        )
        earlier = lax.dynamic_slice_in_dim(carried, offset, block_rows, 1)
        return lax.dynamic_update_slice_in_dim(carried, earlier + contrib, offset, 1)

    partials = lax.fori_loop(0, block_count, add_block, empty)
    summed = lax.psum_scatter(partials, "col", scatter_dimension=1, tiled=True)
    row_terms, kernel_alpha = fold_terms(summed, own_scaled, alpha_rows)
    tile_terms, tile_sum = fold_terms(partials, row_scaled, row_alpha)
    total_rows = row_count * lax.axis_size("row")
    grad = lax.psum(jnp.sum(tile_terms, 1), ("row", "col")) / total_rows
    return (row_terms, kernel_alpha, grad)


def solution(mesh):
    return jax.shard_map(
        on_device,
        mesh=mesh,
        in_specs=(
            P(None, ("row", "col")),
            P(("row", "col")),
            P(None, ("col", "row")),
            P(("col", "row")),
            P(),
        ),
        out_specs=(P(None, ("row", "col")), P(("row", "col")), P()),
        check_vma=False,
    )
```

profile of v0, /device:TPU:0, one launch (start us, length us, event | category | flops | bytes accessed | tf_op | source)
XLA Modules:
  0.0 159.6 jit_solution(6759463865752624172)
XLA Ops:
  7.2 0.7 broadcast_divide_fusion
  7.9 0.8 broadcast_multiply_fusion.2
  8.7 0.7 pad_maximum_fusion.2
  9.3 6.3 %all_gather.7 = f32[17,1024]{1,0:T(8,128)S(1)} all-gather(f32[17,256]{1,0:T(8,128)S(1)} %pad_maximum_fusion.2), channel_id=1, replica_groups=mesh['row'=4,'col'=8] {'row'}, dimensions={1}, use_global_device_ids=true | all-gather | bytes 87040 | tf_op jit(solution)/shard_map/all_gather | solution.py:38
  15.7 0.8 broadcast_multiply_fusion.1
  16.5 0.7 pad_maximum_fusion.1
  17.2 32.0 %all_gather.6 = f32[17,4096]{1,0:T(8,128)S(1)} all-gather(f32[17,512]{1,0:T(8,128)S(1)} %pad_maximum_fusion.1), channel_id=1, replica_groups=mesh['row'=4,'col'=8] {'col'}, dimensions={1}, use_global_device_ids=true | all-gather | bytes 313344 | tf_op jit(solution)/shard_map/all_gather | solution.py:29
  49.4 35.8 %while.13 = (s32[]{:T(128)}, f32[33,4096]{1,0:T(8,128)S(1)}, f32[4096]{0:T(1024)S(1)}, f32[1024]{0:T(1024)S(1)}, f32[16,4096]{1,0:T(8,128)S(1)}, /*index=5*/f32[...) while((s32[]{:T(128)}, f32[33,4096]{1,0:T(8,128)S(1)}, ...), condition=%wide.region_3.0_spmd, body=%wide.region_2.0_spmd.sunk | while | flops 310395392 | bytes 4630695 | solution.py:73
  49.4 1.8 %fusion.40 = f32[512,1024]{1,0:T(8,128)S(1)} fusion(f32[16,1024]{1,0:T(8,128)S(1)} %get-tuple-element.218, f32[16,4096]{1,0:T(8,128)S(1)} %get-tuple-element.217, s32[]{:T(128)S(6)} %select_n.11), kind=kOutput, calls=%fused_computation.13.clone.1 | convolution fusion | flops 100663296 | bytes 2195460 | tf_op jit(solution)/shard_map/while/body/eval_jaxpr/dot_general | solution.py:55
  51.3 2.5 %fusion.41 = f32[33,4096]{1,0:T(8,128)S(1)} fusion(f32[33,4096]{1,0:T(8,128)S(1)} %get-tuple-element.203, s32[]{:T(128)S(6)} %select_n.11, f32[33,1024]{1,0:T(8,128)S(1)} %get-tuple-element.219, f32[512,1024]{1,0:T(8,128)S(1)} %fusion.40, f32[1024]{0:T(1024)S(1)} %get-tuple-element.216, f32[512]{0:T(512)S(1)} %dynamic_slice.29), kind=kOutput, calls=%fused_computation.8.clone.1 | convolution fusion | flops 209732096 | bytes 2430980 | tf_op jit(solution)/shard_map/while/body/eval_jaxpr/dot_general | solution.py:63
  53.9 1.8 %fusion.40 = f32[512,1024]{1,0:T(8,128)S(1)} fusion(f32[16,1024]{1,0:T(8,128)S(1)} %get-tuple-element.218, f32[16,4096]{1,0:T(8,128)S(1)} %get-tuple-element.217, s32[]{:T(128)S(6)} %select_n.11), kind=kOutput, calls=%fused_computation.13.clone.1 | convolution fusion | flops 100663296 | bytes 2195460 | tf_op jit(solution)/shard_map/while/body/eval_jaxpr/dot_general | solution.py:55
  55.8 2.5 %fusion.41 = f32[33,4096]{1,0:T(8,128)S(1)} fusion(f32[33,4096]{1,0:T(8,128)S(1)} %get-tuple-element.203, s32[]{:T(128)S(6)} %select_n.11, f32[33,1024]{1,0:T(8,128)S(1)} %get-tuple-element.219, f32[512,1024]{1,0:T(8,128)S(1)} %fusion.40, f32[1024]{0:T(1024)S(1)} %get-tuple-element.216, f32[512]{0:T(512)S(1)} %dynamic_slice.29), kind=kOutput, calls=%fused_computation.8.clone.1 | convolution fusion | flops 209732096 | bytes 2430980 | tf_op jit(solution)/shard_map/while/body/eval_jaxpr/dot_general | solution.py:63
  58.3 1.8 %fusion.40 = f32[512,1024]{1,0:T(8,128)S(1)} fusion(f32[16,1024]{1,0:T(8,128)S(1)} %get-tuple-element.218, f32[16,4096]{1,0:T(8,128)S(1)} %get-tuple-element.217, s32[]{:T(128)S(6)} %select_n.11), kind=kOutput, calls=%fused_computation.13.clone.1 | convolution fusion | flops 100663296 | bytes 2195460 | tf_op jit(solution)/shard_map/while/body/eval_jaxpr/dot_general | solution.py:55
  60.3 2.5 %fusion.41 = f32[33,4096]{1,0:T(8,128)S(1)} fusion(f32[33,4096]{1,0:T(8,128)S(1)} %get-tuple-element.203, s32[]{:T(128)S(6)} %select_n.11, f32[33,1024]{1,0:T(8,128)S(1)} %get-tuple-element.219, f32[512,1024]{1,0:T(8,128)S(1)} %fusion.40, f32[1024]{0:T(1024)S(1)} %get-tuple-element.216, f32[512]{0:T(512)S(1)} %dynamic_slice.29), kind=kOutput, calls=%fused_computation.8.clone.1 | convolution fusion | flops 209732096 | bytes 2430980 | tf_op jit(solution)/shard_map/while/body/eval_jaxpr/dot_general | solution.py:63
  62.8 1.8 %fusion.40 = f32[512,1024]{1,0:T(8,128)S(1)} fusion(f32[16,1024]{1,0:T(8,128)S(1)} %get-tuple-element.218, f32[16,4096]{1,0:T(8,128)S(1)} %get-tuple-element.217, s32[]{:T(128)S(6)} %select_n.11), kind=kOutput, calls=%fused_computation.13.clone.1 | convolution fusion | flops 100663296 | bytes 2195460 | tf_op jit(solution)/shard_map/while/body/eval_jaxpr/dot_general | solution.py:55
  64.7 2.5 %fusion.41 = f32[33,4096]{1,0:T(8,128)S(1)} fusion(f32[33,4096]{1,0:T(8,128)S(1)} %get-tuple-element.203, s32[]{:T(128)S(6)} %select_n.11, f32[33,1024]{1,0:T(8,128)S(1)} %get-tuple-element.219, f32[512,1024]{1,0:T(8,128)S(1)} %fusion.40, f32[1024]{0:T(1024)S(1)} %get-tuple-element.216, f32[512]{0:T(512)S(1)} %dynamic_slice.29), kind=kOutput, calls=%fused_computation.8.clone.1 | convolution fusion | flops 209732096 | bytes 2430980 | tf_op jit(solution)/shard_map/while/body/eval_jaxpr/dot_general | solution.py:63
  67.3 1.8 %fusion.40 = f32[512,1024]{1,0:T(8,128)S(1)} fusion(f32[16,1024]{1,0:T(8,128)S(1)} %get-tuple-element.218, f32[16,4096]{1,0:T(8,128)S(1)} %get-tuple-element.217, s32[]{:T(128)S(6)} %select_n.11), kind=kOutput, calls=%fused_computation.13.clone.1 | convolution fusion | flops 100663296 | bytes 2195460 | tf_op jit(solution)/shard_map/while/body/eval_jaxpr/dot_general | solution.py:55
  69.2 2.5 %fusion.41 = f32[33,4096]{1,0:T(8,128)S(1)} fusion(f32[33,4096]{1,0:T(8,128)S(1)} %get-tuple-element.203, s32[]{:T(128)S(6)} %select_n.11, f32[33,1024]{1,0:T(8,128)S(1)} %get-tuple-element.219, f32[512,1024]{1,0:T(8,128)S(1)} %fusion.40, f32[1024]{0:T(1024)S(1)} %get-tuple-element.216, f32[512]{0:T(512)S(1)} %dynamic_slice.29), kind=kOutput, calls=%fused_computation.8.clone.1 | convolution fusion | flops 209732096 | bytes 2430980 | tf_op jit(solution)/shard_map/while/body/eval_jaxpr/dot_general | solution.py:63
  71.7 1.8 %fusion.40 = f32[512,1024]{1,0:T(8,128)S(1)} fusion(f32[16,1024]{1,0:T(8,128)S(1)} %get-tuple-element.218, f32[16,4096]{1,0:T(8,128)S(1)} %get-tuple-element.217, s32[]{:T(128)S(6)} %select_n.11), kind=kOutput, calls=%fused_computation.13.clone.1 | convolution fusion | flops 100663296 | bytes 2195460 | tf_op jit(solution)/shard_map/while/body/eval_jaxpr/dot_general | solution.py:55
  73.7 2.5 %fusion.41 = f32[33,4096]{1,0:T(8,128)S(1)} fusion(f32[33,4096]{1,0:T(8,128)S(1)} %get-tuple-element.203, s32[]{:T(128)S(6)} %select_n.11, f32[33,1024]{1,0:T(8,128)S(1)} %get-tuple-element.219, f32[512,1024]{1,0:T(8,128)S(1)} %fusion.40, f32[1024]{0:T(1024)S(1)} %get-tuple-element.216, f32[512]{0:T(512)S(1)} %dynamic_slice.29), kind=kOutput, calls=%fused_computation.8.clone.1 | convolution fusion | flops 209732096 | bytes 2430980 | tf_op jit(solution)/shard_map/while/body/eval_jaxpr/dot_general | solution.py:63
  76.2 1.8 %fusion.40 = f32[512,1024]{1,0:T(8,128)S(1)} fusion(f32[16,1024]{1,0:T(8,128)S(1)} %get-tuple-element.218, f32[16,4096]{1,0:T(8,128)S(1)} %get-tuple-element.217, s32[]{:T(128)S(6)} %select_n.11), kind=kOutput, calls=%fused_computation.13.clone.1 | convolution fusion | flops 100663296 | bytes 2195460 | tf_op jit(solution)/shard_map/while/body/eval_jaxpr/dot_general | solution.py:55
  78.1 2.5 %fusion.41 = f32[33,4096]{1,0:T(8,128)S(1)} fusion(f32[33,4096]{1,0:T(8,128)S(1)} %get-tuple-element.203, s32[]{:T(128)S(6)} %select_n.11, f32[33,1024]{1,0:T(8,128)S(1)} %get-tuple-element.219, f32[512,1024]{1,0:T(8,128)S(1)} %fusion.40, f32[1024]{0:T(1024)S(1)} %get-tuple-element.216, f32[512]{0:T(512)S(1)} %dynamic_slice.29), kind=kOutput, calls=%fused_computation.8.clone.1 | convolution fusion | flops 209732096 | bytes 2430980 | tf_op jit(solution)/shard_map/while/body/eval_jaxpr/dot_general | solution.py:63
  80.7 1.8 %fusion.40 = f32[512,1024]{1,0:T(8,128)S(1)} fusion(f32[16,1024]{1,0:T(8,128)S(1)} %get-tuple-element.218, f32[16,4096]{1,0:T(8,128)S(1)} %get-tuple-element.217, s32[]{:T(128)S(6)} %select_n.11), kind=kOutput, calls=%fused_computation.13.clone.1 | convolution fusion | flops 100663296 | bytes 2195460 | tf_op jit(solution)/shard_map/while/body/eval_jaxpr/dot_general | solution.py:55
  82.6 2.5 %fusion.41 = f32[33,4096]{1,0:T(8,128)S(1)} fusion(f32[33,4096]{1,0:T(8,128)S(1)} %get-tuple-element.203, s32[]{:T(128)S(6)} %select_n.11, f32[33,1024]{1,0:T(8,128)S(1)} %get-tuple-element.219, f32[512,1024]{1,0:T(8,128)S(1)} %fusion.40, f32[1024]{0:T(1024)S(1)} %get-tuple-element.216, f32[512]{0:T(512)S(1)} %dynamic_slice.29), kind=kOutput, calls=%fused_computation.8.clone.1 | convolution fusion | flops 209732096 | bytes 2430980 | tf_op jit(solution)/shard_map/while/body/eval_jaxpr/dot_general | solution.py:63
  85.2 0.8 copy-done
  86.0 0.9 slice.37
  86.9 1.3 multiply_reduce_fusion
  88.3 39.4 %psum.7 = f32[16]{0:T(128)S(1)} all-reduce(f32[16]{0:T(128)S(1)} %multiply_reduce_fusion), channel_id=1, replica_groups=mesh['row'=4,'col'=8] {'row','col'}, use_global_device_ids=true, to_apply=%region_6.0 | all-reduce | flops 16 | bytes 128 | tf_op jit(solution)/shard_map/psum | solution.py:78
  127.7 0.5 broadcast_multiply_fusion.4
  128.2 22.2 %reduce-scatter.2.cloned.1.call-done = f32[33,512]{1,0:T(8,128)} async-done(((f32[33,4096]{1,0:T(8,128)}), f32[33,512]{1,0:T(8,128)}) %reduce-scatter.2.cloned.1.call-update) | async-done | bytes 67600 | tf_op jit(solution)/shard_map/reduce_scatter | solution.py:74
  150.4 0.7 slice.43
  151.2 1.6 fusion.24
  (24 shorter events, 0.9 us)
Async XLA Ops:
  7.2 143.3 %reduce-scatter.2.cloned.1.call-start = ((), (), s32[]{:S(2)}) async-start(), calls=%async_computation.1 | async-start | bytes 737280 | tf_op jit(solution)/shard_map/reduce_scatter | solution.py:74
  49.3 78.8 %copy-start.3 = (f32[512]{0:T(512)S(1)}, f32[512]{0:T(512)}, u32[]{:S(2)}) copy-start(f32[512]{0:T(512)} %param.8) | copy-start | bytes 6148
  49.4 101.8 %copy-start.1 = (f32[16,512]{1,0:T(8,128)S(1)}, f32[16,512]{1,0:T(8,128)}, u32[]{:S(2)}) copy-start(f32[16,512]{1,0:T(8,128)} %param.7) | copy-start | bytes 98308
  85.2 0.8 copy-start
  151.2 1.6 copy-start.2
Sparse Core Ops, SparseCore 0:
  86.1 64.2 reduce-scatter.1
where the time goes:
time: 160 us
  blocking collectives  77.7 us (49%)
  matrix products  34.8 us (22%)
  waiting for transfers between devices  22.3 us (14%)
  between operations  14.1 us (9%)
  other arithmetic  7.18 us (4%)
  local copies, waits for them, and re-layouts  3.16 us (2%)
    psum x1, blocking collectives, on_device(): grad = lax.psum(jnp.sum(tile_terms, 1), ('row', 'col')) / total_rows  39.4 us
    all_gather x1, blocking collectives, on_device(): gathered = lax.all_gather(own_rows, 'col', axis=1, tiled=True)  32 us
    reduce_scatter x1, waiting for transfers between devices, on_device(): summed = lax.psum_scatter(partials, 'col', scatter_dimension=1, tiled=True)  22.2 us
    dot_general x8, matrix products, add_block(): lax.dot_general(values, kernel, (((1,), (1,)), ((), ())), precision=lax.P...  20.1 us
    dot_general x8, matrix products, add_block(): lax.dot_general(row_block, col_scaled, (((0,), (0,)), ((), ())), precisio...  14.7 us
    all_gather x1, blocking collectives, on_device(): shard_piece = lax.all_gather(own_cols, 'row', axis=1, tiled=True)  6.32 us
  transfers between devices with their start and end apart: 1, of which 1 were waited for; matrix products, arithmetic and copies ran while one was open for 2% of the time, Pallas kernels for 0%

commit v1 on v0

v1 whole, which is shorter than its diff:
```python
import functools

import jax
import jax.numpy as jnp
from jax import lax
from jax.experimental import pallas as pl
from jax.experimental.pallas import tpu as pltpu
from jax.sharding import PartitionSpec as P

LOG2E = 1.4426950408889634
CORES = 2
MESH = pl.DeviceIdType.MESH
F32 = jnp.float32
BF16 = jnp.bfloat16


def split3(value):
    high = value.astype(BF16)
    rest = value - high.astype(F32)
    mid = rest.astype(BF16)
    low = (rest - mid.astype(F32)).astype(BF16)
    return high, mid, low


def stack_rows(count, rows):
    index = lax.broadcasted_iota(jnp.int32, (16, count), 0)
    out = jnp.zeros((16, count), F32)
    for place, row in enumerate(rows):
        row = row.astype(F32) if hasattr(row, "astype") else row
        out = jnp.where(index == place, row, out)
    return out.astype(BF16)


def kernel(
    row_size,
    col_size,
    xr_ref,
    ar_ref,
    xc_ref,
    ac_ref,
    ls_ref,
    terms_ref,
    sums_ref,
    grad_ref,
    xg,
    ag,
    acc,
    row_aug,
    part,
    parts,
    send_x,
    recv_x,
    send_a,
    recv_a,
    send_f,
    recv_f,
    send_b,
    recv_b,
    send_g,
    recv_g,
):
    dims, row_count = xr_ref.shape
    col_count = xc_ref.shape[1]
    n_x = row_size // CORES
    n = n_x * col_size
    n_all = row_size * col_size
    my_row = lax.axis_index("row")
    my_col = lax.axis_index("col")
    partner = (my_row + 1 - 2 * (my_row % CORES), my_col)

    def plane_peer(step):
        d_x = step % n_x
        d_col = step // n_x
        return ((my_row + CORES * d_x) % row_size, (my_col + d_col) % col_size)

    def any_peer(step):
        d_row = step % row_size
        d_col = step // row_size
        return ((my_row + d_row) % row_size, (my_col + d_col) % col_size)

    barrier = pltpu.get_barrier_semaphore()

    @pl.loop(1, n_all)
    def _(step):
        pl.semaphore_signal(barrier, inc=1, device_id=any_peer(step), device_id_type=MESH)

    def x_copy(step):
        return pltpu.make_async_remote_copy(
            xc_ref, xg.at[step], send_x.at[step], recv_x.at[step], plane_peer(step), MESH
        )

    def a_copy(step):
        return pltpu.make_async_remote_copy(
            ac_ref, ag.at[step], send_a.at[step], recv_a.at[step], plane_peer(step), MESH
        )

    def x_forward(step, src):
        return pltpu.make_async_remote_copy(
            src, xg.at[n + step], send_f.at[step], recv_f.at[step], partner, MESH
        )

    def a_forward(step, src):
        return pltpu.make_async_remote_copy(
            src, ag.at[n + step], send_b.at[step], recv_b.at[step], partner, MESH
        )

    def g_copy(step):
        return pltpu.make_async_remote_copy(
            part.at[pl.ds(0, 1)],
            parts.at[step],
            send_g.at[step],
            recv_g.at[step],
            any_peer(step),
            MESH,
        )

    eye = lax.broadcasted_iota(jnp.int32, (dims, dims), 0) == lax.broadcasted_iota(
        jnp.int32, (dims, dims), 1
    )
    scale = jnp.sum(jnp.where(eye, jnp.broadcast_to(ls_ref[...], (dims, dims)), 0.0), 1, keepdims=True)
    inverse = 1.0 / scale
    row_scaled = xr_ref[...] * inverse
    row_norm = (-0.5 * LOG2E) * jnp.sum(row_scaled * row_scaled, 0, keepdims=True)
    rh, rm, rl = split3(row_scaled * LOG2E)
    row_aug[...] = jnp.concatenate(
        [rh, rh, rh, rm, rm, rl, stack_rows(row_count, (1.0, 1.0, 1.0) + split3(row_norm))], 0
    )

    def operands(x, alpha):
        scaled = x * inverse
        norm = (-0.5 * LOG2E) * jnp.sum(scaled * scaled, 0, keepdims=True)
        ch, cm, cl = split3(scaled)
        col_aug = jnp.concatenate(
            [ch, cm, cl, ch, cm, ch, stack_rows(col_count, split3(norm) + (1.0, 1.0, 1.0))], 0
        )
        first = alpha * scaled
        fh, fm, fl = split3(first)
        sh, sm, sl = split3(first * scaled)
        group = stack_rows(col_count, split3(alpha))
        zero = jnp.zeros_like(fl)
        left_high = jnp.concatenate([fh, sh, fm, sm, fl, sl, group], 0)
        left_mid = jnp.concatenate([fh, sh, fm, sm, zero, zero, group], 0)
        exponent = lax.dot_general(
            col_aug, row_aug[...], (((0,), (0,)), ((), ())), preferred_element_type=F32
        )
        value = jnp.exp2(exponent)
        high = value.astype(BF16)
        mid = (value - high.astype(F32)).astype(BF16)
        return [left_high, left_mid], [high, mid]

    def contribute(chunks):
        left, right = [], []
        for x, alpha in chunks:
            more_left, more_right = operands(x, alpha)
            left += more_left
            right += more_right
        return jnp.dot(
            jnp.concatenate(left, 1), jnp.concatenate(right, 0), preferred_element_type=F32
        )

    acc[...] = contribute([(xc_ref[...], ac_ref[...])])

    pl.semaphore_wait(barrier, n_all - 1)
    x_forward(0, xc_ref).start()
    a_forward(0, ac_ref).start()

    @pl.loop(1, n)
    def _(step):
        x_copy(step).start()
        a_copy(step).start()

    @pl.loop(1, n)
    def _(step):
        x_copy(step).wait_recv()
        a_copy(step).wait_recv()
        x_forward(step, xg.at[step]).start()
        a_forward(step, ag.at[step]).start()
        x_forward(step - 1, xg.at[step]).wait_recv()
        a_forward(step - 1, ag.at[step]).wait_recv()
        acc[...] += contribute(
            [(xg[step], ag[step]), (xg[n + step - 1], ag[n + step - 1])]
        )

    x_forward(n - 1, xc_ref).wait_recv()
    a_forward(n - 1, ac_ref).wait_recv()
    total = acc[...] + contribute([(xg[2 * n - 1], ag[2 * n - 1])])
    first = total[0:16] + total[32:48] + total[64:80]
    second = total[16:32] + total[48:64] + total[80:96]
    weight = total[96:97] + total[97:98] + total[98:99]
    terms = (0.5 * ar_ref[...]) * (
        row_scaled * row_scaled * weight - 2.0 * row_scaled * first + second
    )
    folded = terms[:, 0:128]
    for at in range(128, row_count, 128):
        folded = folded + terms[:, at : at + 128]
    gathered = lax.dot_general(
        jnp.ones((8, 128), F32),
        folded,
        (((1,), (1,)), ((), ())),
        precision=lax.Precision.HIGHEST,
        preferred_element_type=F32,
    )
    part[...] = jnp.zeros_like(part)
    part[:, 0:dims] = gathered
    terms_ref[...] = terms
    sums_ref[...] = weight

    @pl.loop(1, n)
    def _(step):
        x_copy(step).wait_send()
        a_copy(step).wait_send()

    @pl.loop(0, n)
    def _(step):
        x_forward(step, xc_ref).wait_send()
        a_forward(step, ac_ref).wait_send()

    @pl.loop(1, n_all)
    def _(step):
        g_copy(step).start()

    parts[0] = part[0:1]

    @pl.loop(1, n_all)
    def _(step):
        g_copy(step).wait()

    grad_ref[...] = (jnp.sum(parts[...], 0) / (row_count * n_all))[:, 0:dims]


def on_device(row_size, col_size, x_rows, alpha_rows, x_cols, alpha_cols, lengthscale):
    dims, row_count = x_rows.shape
    col_count = x_cols.shape[1]
    n = row_size // CORES * col_size
    n_all = row_size * col_size
    vmem = pl.BlockSpec(memory_space=pltpu.VMEM)
    dma = pltpu.SemaphoreType.DMA
    terms, sums, grad = pl.pallas_call(
        functools.partial(kernel, row_size, col_size),
        out_shape=(
            jax.ShapeDtypeStruct((dims, row_count), F32),
            jax.ShapeDtypeStruct((1, row_count), F32),
            jax.ShapeDtypeStruct((1, dims), F32),
        ),
        in_specs=[vmem] * 5,
        out_specs=(vmem, vmem, vmem),
        scratch_shapes=[
            pltpu.VMEM((2 * n, dims, col_count), F32),
            pltpu.VMEM((2 * n, 1, col_count), F32),
            pltpu.VMEM((112, row_count), F32),
            pltpu.VMEM((112, row_count), BF16),
            pltpu.VMEM((8, 128), F32),
            pltpu.VMEM((n_all, 1, 128), F32),
        ]
        + [dma((n,))] * 8
        + [dma((n_all,))] * 2,
        compiler_params=pltpu.CompilerParams(collective_id=0, has_side_effects=True),
    )(
        x_rows,
        alpha_rows.reshape(1, row_count),
        x_cols,
        alpha_cols.reshape(1, col_count),
        lengthscale.reshape(1, dims),
    )
    return terms, sums.reshape(row_count), grad.reshape(dims)


def solution(mesh):
    return jax.shard_map(
        functools.partial(on_device, mesh.shape["row"], mesh.shape["col"]),
        mesh=mesh,
        in_specs=(
            P(None, ("row", "col")),
            P(("row", "col")),
            P(None, ("col", "row")),
            P(("col", "row")),
            P(),
        ),
        out_specs=(P(None, ("row", "col")), P(("row", "col")), P()),
        check_vma=False,
    )
```

time: 160 us -> 33.5 us (0.21)
  blocking collectives: 77.7 us -> 0 us
  matrix products: 34.8 us -> 0 us
  Pallas kernels: 0 us -> 30.1 us
  waiting for transfers between devices: 22.3 us -> 0 us
  between operations: 14.1 us -> 0.65 us
  other arithmetic: 7.18 us -> 0 us
    psum x1 -> x0, blocking collectives: 39.4 us -> none  [on_device(): grad = lax.psum(jnp.sum(tile_terms, 1), ('row', 'col')) / total_rows]
    all_gather x2 -> x0, blocking collectives: 38.3 us -> none  [the longest x1 32 us: on_device(): gathered = lax.all_gather(own_rows, 'col', axis=1, tiled=True)]
    dot_general x16 -> x0, matrix products: 34.8 us -> none  [the longest x8 20.1 us: add_block(): lax.dot_general(values, kernel, (((1,), (1,)), ((), ())), precision=lax.P...]
    pallas_call x0 -> x1, Pallas kernels: none -> 30.1 us  [on_device(): pl.pallas_call(functools.partial(kernel, row_size, col_size), out_shape=(...]
    reduce_scatter x1 -> x0, waiting for transfers between devices: 22.2 us -> none  [on_device(): summed = lax.psum_scatter(partials, 'col', scatter_dimension=1, tiled=True)]
    mul x6 -> x0, other arithmetic: 3.23 us -> none  [the longest x3 1.58 us: fold_terms(): 0.5 * row_alpha[None, :]]
    unnamed x8 -> x7, local copies, waits for them, and re-layouts: 0.84 us -> 2.49 us
    slice x3 -> x0, local copies, waits for them, and re-layouts: 1.64 us -> none  [the longest x2 1.63 us: fold_terms(): weight_sum = partials[0]]
  transfers between devices with their start and end apart: 1 -> 0, of which waited for: 1 -> 0; matrix products, arithmetic and copies ran while one was open for 2% -> 0% of each run, Pallas kernels for 0% -> 0%
where the time goes in v1:
time: 33.5 us; the launch traced here: 33.2 us
  Pallas kernels  30.1 us (90%)
  local copies, waits for them, and re-layouts  2.49 us (7%)
  between operations  0.65 us (2%)
    pallas_call x1, Pallas kernels, on_device(): pl.pallas_call(functools.partial(kernel, row_size, col_size), out_shape=(...  30.1 us
    unnamed x7, local copies, waits for them, and re-layouts  2.49 us

profile of v1, /device:TPU:0, one launch (start us, length us, event | category | flops | bytes accessed | tf_op | source)
XLA Modules:
  0.0 33.2 jit_solution(13829811977184573255)
XLA Ops:
  0.6 30.1 %shard_map.76 = (f32[16,512]{1,0:T(8,128)}, f32[1,512]{1,0:T(1,128)}, f32[1,16]{1,0:T(1,128)}) custom-call(f32[16,512]{1,0:T(8,128)} %xr_ref.1, f32[1,512]{1,0:T(1,128)} %bitcast.5, f32[16,256]{1,0:T(8,128)} %xc_ref.1, f32[1,256]{1,0:T(1,128)} %bitcast.7, f32[1,16]{1,0:T(1,128)} %bitcast.8), custom_call_target="tpu_custom_call" | custom-call | tf_op jit(solution)/shard_map/pallas_call | solution.py:238
  30.7 0.0 copy-start
  30.7 1.4 %copy.11 = f32[16,512]{1,0:T(8,128)} copy(f32[16,512]{1,0:T(8,128)} %get-tuple-element.12) | data formatting | bytes 65536
  32.1 0.0 copy-done
  32.1 0.0 copy-start.1
  32.1 0.6 %copy.12 = f32[512]{0:T(512)} copy(f32[512]{0:T(512)S(1)} %bitcast.6) | data formatting | bytes 4096
  32.7 0.0 copy-done.1
  32.7 0.5 %copy.13 = f32[16]{0:T(128)} copy(f32[16]{0:T(128)S(1)} %bitcast.9) | data formatting | bytes 128
Async XLA Ops:
  30.7 1.4 %copy-start = (f32[1,512]{1,0:T(1,128)S(1)}, f32[1,512]{1,0:T(1,128)}, u32[]{:S(2)}) copy-start(f32[1,512]{1,0:T(1,128)} %get-tuple-element.7) | copy-start | bytes 6148
  32.1 0.6 %copy-start.1 = (f32[1,16]{1,0:T(1,128)S(1)}, f32[1,16]{1,0:T(1,128)}, u32[]{:S(2)}) copy-start(f32[1,16]{1,0:T(1,128)} %get-tuple-element.8) | copy-start | bytes 196

commit v2 on v1

--- a/solution.py
+++ b/solution.py
@@ -34,74 +34,99 @@
 def kernel(
     row_size,
     col_size,
+    xr_hbm,
+    ar_hbm,
+    xc_hbm,
+    ac_hbm,
+    ls_hbm,
+    terms_hbm,
+    sums_hbm,
+    grad_hbm,
     xr_ref,
     ar_ref,
-    xc_ref,
-    ac_ref,
     ls_ref,
     terms_ref,
     sums_ref,
     grad_ref,
-    xg,
-    ag,
+    chunks,
     acc,
     row_aug,
     part,
     parts,
-    send_x,
-    recv_x,
-    send_a,
-    recv_a,
+    local,
+    send_c,
+    recv_c,
     send_f,
     recv_f,
-    send_b,
-    recv_b,
     send_g,
     recv_g,
 ):
     dims, row_count = xr_ref.shape
-    col_count = xc_ref.shape[1]
+    col_count = chunks.shape[2]
     n_x = row_size // CORES
+    n_y = n_x if col_size % n_x == 0 else 1
+    n_z = col_size // n_y
+    n_plane = n_x * n_y
     n = n_x * col_size
     n_all = row_size * col_size
     my_row = lax.axis_index("row")
     my_col = lax.axis_index("col")
+    my_z = my_col // n_y
+    my_y = my_col % n_y
     partner = (my_row + 1 - 2 * (my_row % CORES), my_col)
 
-    def plane_peer(step):
-        d_x = step % n_x
-        d_col = step // n_x
-        return ((my_row + CORES * d_x) % row_size, (my_col + d_col) % col_size)
+    def line_peer(j):
+        return (my_row, (my_z + j) % n_z * n_y + my_y)
+
+    def plane_peer(m):
+        return (
+            (my_row + CORES * (m % n_x)) % row_size,
+            my_z * n_y + (my_y + m // n_x) % n_y,
+        )
 
     def any_peer(step):
         d_row = step % row_size
         d_col = step // row_size
         return ((my_row + d_row) % row_size, (my_col + d_col) % col_size)
 
+    def loads():
+        return [
+            pltpu.make_async_copy(xc_hbm, chunks.at[0, pl.ds(0, dims)], local.at[0]),
+            pltpu.make_async_copy(ac_hbm, chunks.at[0, pl.ds(dims, 1)], local.at[1]),
+            pltpu.make_async_copy(xr_hbm, xr_ref, local.at[2]),
+            pltpu.make_async_copy(ar_hbm, ar_ref, local.at[3]),
+            pltpu.make_async_copy(ls_hbm, ls_ref, local.at[4]),
+        ]
+
+    for copy in loads():
+        copy.start()
+
     barrier = pltpu.get_barrier_semaphore()
 
-    @pl.loop(1, n_all)
-    def _(step):
-        pl.semaphore_signal(barrier, inc=1, device_id=any_peer(step), device_id_type=MESH)
-
-    def x_copy(step):
+    pl.semaphore_signal(barrier, inc=1, device_id=partner, device_id_type=MESH)
+
+    @pl.loop(1, n_plane)
+    def _(m):
+        pl.semaphore_signal(barrier, inc=1, device_id=plane_peer(m), device_id_type=MESH)
+
+    @pl.loop(1, n_z)
+    def _(j):
+        pl.semaphore_signal(barrier, inc=1, device_id=line_peer(j), device_id_type=MESH)
+
+    def line_copy(j):
         return pltpu.make_async_remote_copy(
-            xc_ref, xg.at[step], send_x.at[step], recv_x.at[step], plane_peer(step), MESH
-        )
-
-    def a_copy(step):
+            chunks.at[0], chunks.at[j], send_c.at[j], recv_c.at[j], line_peer(j), MESH
+        )
+
+    def plane_copy(j, m):
+        slot = m * n_z + j
         return pltpu.make_async_remote_copy(
-            ac_ref, ag.at[step], send_a.at[step], recv_a.at[step], plane_peer(step), MESH
-        )
-
-    def x_forward(step, src):
+            chunks.at[j], chunks.at[slot], send_c.at[slot], recv_c.at[slot], plane_peer(m), MESH
+        )
+
+    def forward(slot):
         return pltpu.make_async_remote_copy(
-            src, xg.at[n + step], send_f.at[step], recv_f.at[step], partner, MESH
-        )
-
-    def a_forward(step, src):
-        return pltpu.make_async_remote_copy(
-            src, ag.at[n + step], send_b.at[step], recv_b.at[step], partner, MESH
+            chunks.at[slot], chunks.at[n + slot], send_f.at[slot], recv_f.at[slot], partner, MESH
         )
 
     def g_copy(step):
@@ -113,6 +138,9 @@
             any_peer(step),
             MESH,
         )
+
+    for copy in loads():
+        copy.wait()
 
     eye = lax.broadcasted_iota(jnp.int32, (dims, dims), 0) == lax.broadcasted_iota(
         jnp.int32, (dims, dims), 1
@@ -148,42 +176,60 @@
         mid = (value - high.astype(F32)).astype(BF16)
         return [left_high, left_mid], [high, mid]
 
-    def contribute(chunks):
+    def contribute(slots):
         left, right = [], []
-        for x, alpha in chunks:
-            more_left, more_right = operands(x, alpha)
+        for slot in slots:
+            more_left, more_right = operands(
+                chunks[slot, 0:dims], chunks[slot, dims : dims + 1]
+            )
             left += more_left
             right += more_right
         return jnp.dot(
             jnp.concatenate(left, 1), jnp.concatenate(right, 0), preferred_element_type=F32
         )
 
-    acc[...] = contribute([(xc_ref[...], ac_ref[...])])
-
-    pl.semaphore_wait(barrier, n_all - 1)
-    x_forward(0, xc_ref).start()
-    a_forward(0, ac_ref).start()
-
-    @pl.loop(1, n)
-    def _(step):
-        x_copy(step).start()
-        a_copy(step).start()
-
-    @pl.loop(1, n)
-    def _(step):
-        x_copy(step).wait_recv()
-        a_copy(step).wait_recv()
-        x_forward(step, xg.at[step]).start()
-        a_forward(step, ag.at[step]).start()
-        x_forward(step - 1, xg.at[step]).wait_recv()
-        a_forward(step - 1, ag.at[step]).wait_recv()
-        acc[...] += contribute(
-            [(xg[step], ag[step]), (xg[n + step - 1], ag[n + step - 1])]
-        )
-
-    x_forward(n - 1, xc_ref).wait_recv()
-    a_forward(n - 1, ac_ref).wait_recv()
-    total = acc[...] + contribute([(xg[2 * n - 1], ag[2 * n - 1])])
+    acc[...] = contribute([0])
+
+    pl.semaphore_wait(barrier, n_plane + n_z - 1)
+
+    @pl.loop(1, n_z)
+    def _(j):
+        line_copy(j).start()
+
+    @pl.loop(1, n_plane)
+    def _(m):
+        plane_copy(0, m).start()
+
+    forward(0).start()
+    forward(0).wait_recv()
+    acc[...] += contribute([n])
+
+    @pl.loop(1, n_z)
+    def _(j):
+        line_copy(j).wait_recv()
+
+        @pl.loop(1, n_plane)
+        def _(m):
+            plane_copy(j, m).start()
+
+        forward(j).start()
+        acc[...] += contribute([j])
+
+    lag = n_z - 1
+
+    @pl.loop(n_z, n)
+    def _(slot):
+        line_copy(slot).wait_recv()
+        forward(slot).start()
+        forward(slot - lag).wait_recv()
+        acc[...] += contribute([slot, n + slot - lag])
+
+    @pl.loop(n - lag, n)
+    def _(slot):
+        forward(slot).wait_recv()
+        acc[...] += contribute([n + slot])
+
+    total = acc[...]
     first = total[0:16] + total[32:48] + total[64:80]
     second = total[16:32] + total[48:64] + total[80:96]
     weight = total[96:97] + total[97:98] + total[98:99]
@@ -205,20 +251,27 @@
     terms_ref[...] = terms
     sums_ref[...] = weight
 
-    @pl.loop(1, n)
-    def _(step):
-        x_copy(step).wait_send()
-        a_copy(step).wait_send()
-
-    @pl.loop(0, n)
-    def _(step):
-        x_forward(step, xc_ref).wait_send()
-        a_forward(step, ac_ref).wait_send()
+    stores = [
+        pltpu.make_async_copy(terms_ref, terms_hbm, local.at[0]),
+        pltpu.make_async_copy(sums_ref, sums_hbm, local.at[1]),
+    ]
+    for copy in stores:
+        copy.start()
 
     @pl.loop(1, n_all)
     def _(step):
         g_copy(step).start()
 
+    @pl.loop(1, n)
+    def _(slot):
+        line_copy(slot).wait_send()
+
+    @pl.loop(0, n)
+    def _(slot):
+        forward(slot).wait_send()
+
+    for copy in stores:
+        copy.wait()
     parts[0] = part[0:1]
 
     @pl.loop(1, n_all)
@@ -226,6 +279,9 @@
         g_copy(step).wait()
 
     grad_ref[...] = (jnp.sum(parts[...], 0) / (row_count * n_all))[:, 0:dims]
+    copy = pltpu.make_async_copy(grad_ref, grad_hbm, local.at[2])
+    copy.start()
+    copy.wait()
 
 
 def on_device(row_size, col_size, x_rows, alpha_rows, x_cols, alpha_cols, lengthscale):
@@ -233,7 +289,7 @@
     col_count = x_cols.shape[1]
     n = row_size // CORES * col_size
     n_all = row_size * col_size
-    vmem = pl.BlockSpec(memory_space=pltpu.VMEM)
+    anywhere = pl.BlockSpec(memory_space=pl.ANY)
     dma = pltpu.SemaphoreType.DMA
     terms, sums, grad = pl.pallas_call(
         functools.partial(kernel, row_size, col_size),
@@ -242,17 +298,23 @@
             jax.ShapeDtypeStruct((1, row_count), F32),
             jax.ShapeDtypeStruct((1, dims), F32),
         ),
-        in_specs=[vmem] * 5,
-        out_specs=(vmem, vmem, vmem),
+        in_specs=[anywhere] * 5,
+        out_specs=(anywhere, anywhere, anywhere),
         scratch_shapes=[
-            pltpu.VMEM((2 * n, dims, col_count), F32),
-            pltpu.VMEM((2 * n, 1, col_count), F32),
+            pltpu.VMEM((dims, row_count), F32),
+            pltpu.VMEM((1, row_count), F32),
+            pltpu.VMEM((1, dims), F32),
+            pltpu.VMEM((dims, row_count), F32),
+            pltpu.VMEM((1, row_count), F32),
+            pltpu.VMEM((1, dims), F32),
+            pltpu.VMEM((2 * n, dims + 1, col_count), F32),
             pltpu.VMEM((112, row_count), F32),
             pltpu.VMEM((112, row_count), BF16),
             pltpu.VMEM((8, 128), F32),
             pltpu.VMEM((n_all, 1, 128), F32),
+            dma((5,)),
         ]
-        + [dma((n,))] * 8
+        + [dma((n,))] * 4
         + [dma((n_all,))] * 2,
         compiler_params=pltpu.CompilerParams(collective_id=0, has_side_effects=True),
     )(

time: 33.5 us -> 29.3 us (0.87)
  Pallas kernels: 30.1 us -> 25.9 us
    pallas_call x1, Pallas kernels: 30.1 us -> 25.9 us  [on_device(): pl.pallas_call(functools.partial(kernel, row_size, col_size), out_shape=(...]
where the time goes in v2:
time: 29.3 us; the launch traced here: 29 us
  Pallas kernels  25.9 us (88%)
  local copies, waits for them, and re-layouts  2.49 us (8%)
  between operations  0.65 us (2%)
    pallas_call x1, Pallas kernels, on_device(): pl.pallas_call(functools.partial(kernel, row_size, col_size), out_shape=(...  25.9 us
    unnamed x7, local copies, waits for them, and re-layouts  2.49 us

profile of v2, /device:TPU:0, one launch (start us, length us, event | category | flops | bytes accessed | tf_op | source)
XLA Modules:
  0.0 29.0 jit_solution(6546403167863403501)
XLA Ops:
  0.6 25.9 %shard_map.76 = (f32[16,512]{1,0:T(8,128)}, f32[1,512]{1,0:T(1,128)}, f32[1,16]{1,0:T(1,128)}) custom-call(f32[16,512]{1,0:T(8,128)} %xr_hbm.1, f32[1,512]{1,0:T(1,128)} %bitcast.5, f32[16,256]{1,0:T(8,128)} %xc_hbm.1, f32[1,256]{1,0:T(1,128)} %bitcast.7, f32[1,16]{1,0:T(1,128)} %bitcast.8), custom_call_target="tpu_custom_call" | custom-call | tf_op jit(solution)/shard_map/pallas_call | solution.py:294
  26.5 0.0 copy-start
  26.5 1.4 %copy.11 = f32[16,512]{1,0:T(8,128)} copy(f32[16,512]{1,0:T(8,128)} %get-tuple-element.12) | data formatting | bytes 65536
  27.9 0.0 copy-done
  27.9 0.0 copy-start.1
  27.9 0.6 %copy.12 = f32[512]{0:T(512)} copy(f32[512]{0:T(512)S(1)} %bitcast.6) | data formatting | bytes 4096
  28.5 0.0 copy-done.1
  28.5 0.5 %copy.13 = f32[16]{0:T(128)} copy(f32[16]{0:T(128)S(1)} %bitcast.9) | data formatting | bytes 128
Async XLA Ops:
  26.5 1.4 %copy-start = (f32[1,512]{1,0:T(1,128)S(1)}, f32[1,512]{1,0:T(1,128)}, u32[]{:S(2)}) copy-start(f32[1,512]{1,0:T(1,128)} %get-tuple-element.7) | copy-start | bytes 6148
  27.9 0.6 %copy-start.1 = (f32[1,16]{1,0:T(1,128)S(1)}, f32[1,16]{1,0:T(1,128)}, u32[]{:S(2)}) copy-start(f32[1,16]{1,0:T(1,128)} %get-tuple-element.8) | copy-start | bytes 196

commit v3 on v2

--- a/solution.py
+++ b/solution.py
@@ -188,6 +188,12 @@
             jnp.concatenate(left, 1), jnp.concatenate(right, 0), preferred_element_type=F32
         )
 
+    def in_groups(slots):
+        slots = list(slots)
+        for at in range(0, len(slots), 4):
+            acc[...] += contribute(slots[at : at + 4])
+
+    width = 2 if (n - n_z) % 2 == 0 else 1
     acc[...] = contribute([0])
 
     pl.semaphore_wait(barrier, n_plane + n_z - 1)
@@ -201,8 +207,6 @@
         plane_copy(0, m).start()
 
     forward(0).start()
-    forward(0).wait_recv()
-    acc[...] += contribute([n])
 
     @pl.loop(1, n_z)
     def _(j):
@@ -213,21 +217,26 @@
             plane_copy(j, m).start()
 
         forward(j).start()
-        acc[...] += contribute([j])
-
+
+    forward(0).wait_recv()
     lag = n_z - 1
-
-    @pl.loop(n_z, n)
-    def _(slot):
-        line_copy(slot).wait_recv()
-        forward(slot).start()
-        forward(slot - lag).wait_recv()
-        acc[...] += contribute([slot, n + slot - lag])
+    in_groups([n] + list(range(1, n_z)))
+
+    @pl.loop(0, (n - n_z) // width)
+    def _(group):
+        slots = [n_z + group * width + k for k in range(width)]
+        for slot in slots:
+            line_copy(slot).wait_recv()
+            forward(slot).start()
+        for slot in slots:
+            forward(slot - lag).wait_recv()
+        acc[...] += contribute(slots + [n + slot - lag for slot in slots])
 
     @pl.loop(n - lag, n)
     def _(slot):
         forward(slot).wait_recv()
-        acc[...] += contribute([n + slot])
+
+    in_groups(range(2 * n - lag, 2 * n))
 
     total = acc[...]
     first = total[0:16] + total[32:48] + total[64:80]

time: 29.3 us -> 27.7 us (0.945)
  Pallas kernels: 25.9 us -> 24.3 us
    pallas_call x1, Pallas kernels: 25.9 us -> 24.3 us  [on_device(): pl.pallas_call(functools.partial(kernel, row_size, col_size), out_shape=(...]
where the time goes in v3:
time: 27.7 us; the launch traced here: 27.5 us
  Pallas kernels  24.3 us (88%)
  local copies, waits for them, and re-layouts  2.49 us (9%)
  between operations  0.65 us (2%)
    pallas_call x1, Pallas kernels, on_device(): pl.pallas_call(functools.partial(kernel, row_size, col_size), out_shape=(...  24.3 us
    unnamed x7, local copies, waits for them, and re-layouts  2.49 us

profile of v3, /device:TPU:0, one launch (start us, length us, event | category | flops | bytes accessed | tf_op | source)
XLA Modules:
  0.0 27.5 jit_solution(17298536130929779511)
XLA Ops:
  0.6 24.3 %shard_map.76 = (f32[16,512]{1,0:T(8,128)}, f32[1,512]{1,0:T(1,128)}, f32[1,16]{1,0:T(1,128)}) custom-call(f32[16,512]{1,0:T(8,128)} %xr_hbm.1, f32[1,512]{1,0:T(1,128)} %bitcast.5, f32[16,256]{1,0:T(8,128)} %xc_hbm.1, f32[1,256]{1,0:T(1,128)} %bitcast.7, f32[1,16]{1,0:T(1,128)} %bitcast.8), custom_call_target="tpu_custom_call" | custom-call | tf_op jit(solution)/shard_map/pallas_call | solution.py:303
  25.0 0.0 copy-start
  25.0 1.4 %copy.11 = f32[16,512]{1,0:T(8,128)} copy(f32[16,512]{1,0:T(8,128)} %get-tuple-element.12) | data formatting | bytes 65536
  26.4 0.0 copy-done
  26.4 0.0 copy-start.1
  26.4 0.6 %copy.12 = f32[512]{0:T(512)} copy(f32[512]{0:T(512)S(1)} %bitcast.6) | data formatting | bytes 4096
  26.9 0.0 copy-done.1
  27.0 0.5 %copy.13 = f32[16]{0:T(128)} copy(f32[16]{0:T(128)S(1)} %bitcast.9) | data formatting | bytes 128
Async XLA Ops:
  25.0 1.4 %copy-start = (f32[1,512]{1,0:T(1,128)S(1)}, f32[1,512]{1,0:T(1,128)}, u32[]{:S(2)}) copy-start(f32[1,512]{1,0:T(1,128)} %get-tuple-element.7) | copy-start | bytes 6148
  26.4 0.6 %copy-start.1 = (f32[1,16]{1,0:T(1,128)S(1)}, f32[1,16]{1,0:T(1,128)}, u32[]{:S(2)}) copy-start(f32[1,16]{1,0:T(1,128)} %get-tuple-element.8) | copy-start | bytes 196

commit v4 on v3

--- a/solution.py
+++ b/solution.py
@@ -293,11 +293,18 @@
     copy.wait()
 
 
+def settle(terms_in, sums_in, grad_in, terms_out, sums_out, grad_out):
+    terms_out[...] = terms_in[...]
+    sums_out[...] = sums_in[...]
+    grad_out[...] = grad_in[...]
+
+
 def on_device(row_size, col_size, x_rows, alpha_rows, x_cols, alpha_cols, lengthscale):
     dims, row_count = x_rows.shape
     col_count = x_cols.shape[1]
     n = row_size // CORES * col_size
     n_all = row_size * col_size
+    vmem = pl.BlockSpec(memory_space=pltpu.VMEM)
     anywhere = pl.BlockSpec(memory_space=pl.ANY)
     dma = pltpu.SemaphoreType.DMA
     terms, sums, grad = pl.pallas_call(
@@ -333,6 +340,12 @@
         alpha_cols.reshape(1, col_count),
         lengthscale.reshape(1, dims),
     )
+    terms, sums, grad = pl.pallas_call(
+        settle,
+        out_shape=(terms, sums, grad),
+        in_specs=[vmem] * 3,
+        out_specs=(vmem, vmem, vmem),
+    )(terms, sums, grad)
     return terms, sums.reshape(row_count), grad.reshape(dims)
 
 

time: 27.7 us -> 26.6 us (0.960)
  local copies, waits for them, and re-layouts: 2.49 us -> 0 us
  Pallas kernels: 24.3 us -> 25.7 us
    unnamed x7 -> x0, local copies, waits for them, and re-layouts: 2.49 us -> none
    pallas_call x0 -> x1, Pallas kernels: none -> 1.39 us  [on_device(): pl.pallas_call(settle, out_shape=(terms, sums, grad), in_specs=[vmem] * 3...]
where the time goes in v4:
time: 26.6 us; the launch traced here: 26.4 us
  Pallas kernels  25.7 us (97%)
  between operations  0.64 us (2%)
    pallas_call x1, Pallas kernels, on_device(): pl.pallas_call(functools.partial(kernel, row_size, col_size), out_shape=(...  24.3 us
    pallas_call x1, Pallas kernels, on_device(): pl.pallas_call(settle, out_shape=(terms, sums, grad), in_specs=[vmem] * 3...  1.39 us

profile of v4, /device:TPU:0, one launch (start us, length us, event | category | flops | bytes accessed | tf_op | source)
XLA Modules:
  0.0 26.4 jit_solution(62758965822554039)
XLA Ops:
  0.6 24.3 %shard_map.76 = (f32[16,512]{1,0:T(8,128)}, f32[1,512]{1,0:T(1,128)}, f32[1,16]{1,0:T(1,128)}) custom-call(f32[16,512]{1,0:T(8,128)} %xr_hbm.1, f32[1,512]{1,0:T(1,128)} %bitcast.5, f32[16,256]{1,0:T(8,128)} %xc_hbm.1, f32[1,256]{1,0:T(1,128)} %bitcast.6, f32[1,16]{1,0:T(1,128)} %bitcast.7), custom_call_target="tpu_custom_call" | custom-call | tf_op jit(solution)/shard_map/pallas_call | solution.py:310
  25.0 1.4 %shard_map.77 = (f32[16,512]{1,0:T(8,128)}, f32[1,512]{1,0:T(1,128)}, f32[1,16]{1,0:T(1,128)}) custom-call(f32[16,512]{1,0:T(8,128)} %get-tuple-element.9.terms_in, f32[1,512]{1,0:T(1,128)} %get-tuple-element.10.sums_in, f32[1,16]{1,0:T(1,128)} %get-tuple-element.11.grad_in), custom_call_target="tpu_custom_call" | custom-call | tf_op jit(solution)/shard_map/pallas_call | solution.py:343
